TPU v7x, 32 devices: a whole 2x2x4 slice. The times are simulated.
32 devices in a mesh: gx: 4 (over y, x), gy: 8 (over z, core).
Axes of the slice: x: 2, y: 2, z: 4, core: 2. Of those that a mesh axis runs over, the one named last changes fastest.
Arguments:
- primal: float32 [4, 27, 16384], P(None, None, ('gx', 'gy')), may hold values from -6 to 6
- adjoint: float32 [4, 27, 16384], P(None, None, ('gx', 'gy')), may hold values from -6 to 6
- source: float32 [4, 27, 16384], P(None, None, ('gx', 'gy')), may hold values from -6 to 6
- coefficient: float32 [16384], P(('gx', 'gy')), may hold values from 0.3 to 3
- levels: int32 [16384], P(('gx', 'gy')), may hold values from 0 to 3
- recon: float32 [7, 125, 27], replicated, may hold values from -0.4375 to 0.4375
- stiffness: float32 [125, 27], replicated, may hold values from -1.25 to 1.25
- interp: float32 [125, 27], replicated, may hold values from -1.25 to 1.25
- flux: float32 [6, 25, 27], replicated, may hold values from -1.25 to 1.25
- face_eval: float32 [6, 25, 125], replicated, may hold values from -0.5 to 0.5
- child_interp: float32 [4, 25, 25], replicated, may hold values from -1.25 to 1.25
- ghost_send: int32 [32, 8, 32], P(('gx', 'gy')), may hold values from -1 to 511, as said below
- edge_send: int32 [32, 2, 16], P(('gx', 'gy')), may hold values from -1 to 511, as said below
- neighbor_slot: int32 [6, 16384], P(None, ('gx', 'gy')), may hold values from -1 to 799, as said below
- neighbor_child: int32 [6, 16384], P(None, ('gx', 'gy')), may hold values from 0 to 4, as said below
- hang_send: int32 [2, 32, 8, 8], P(None, ('gx', 'gy')), may hold values from -1 to 511, as said below
- hang_recv: int32 [3, 32, 8, 8], P(None, ('gx', 'gy')), may hold values from -1 to 511, as said below
Outputs:
- cell_indicator: float32 [4, 16384], P(None, ('gx', 'gy'))
- face_indicator: float32 [4, 16384], P(None, ('gx', 'gy'))
Inputs may be any that keep to these rules, and one draw needn't show every extreme that they name: `ghost_send`: the gy index of a device numbers a block of a cube of blocks with side S, the cube root of 8: index = G(c0) + S * G(c1) + S * S * G(c2) for block coordinates c0, c1, c2, where G(p) = p xor (p // 2) is the Gray code, so face-adjacent blocks differ in one bit of the index. Row [r, p] lists the local cells that device r sends to the device with its gx index and gy index p, live ids first, then -1. Only the up to six blocks face-adjacent to r's block get live ids, between 16 and 32 of them, and exactly 32 go to the neighbour one step up along coordinate 0 wherever it exists. `edge_send`: row [r, 0] lists the local cells sent to the device one gx index lower with the same gy index, row [r, 1] those sent to the one higher, live ids first, then -1; where that device exists there are 8 to 16 live ids, and exactly 16 towards the lower one; otherwise the row is all -1. `neighbor_slot`: every slot that is not -1 points at a live entry: a cell of the device itself, a live entry of a gy peer's ghost_send row for this device, or a live entry of a gx neighbour's edge_send row towards this device. `neighbor_child`: 4 means a neighbour of the same level. `hang_send`: [0, r, p, t] is a local cell of device r and [1, r, p, t] one of its faces, both -1 after the live slots; live slots go only to face-adjacent gy peers (as for ghost_send), at most 8 to one peer, and the device with gy index 0 sends exactly 8 to each of its face-adjacent peers. `hang_recv`: [:, q, p, t] describes what device q receives in slot t from the device with its gx index and gy index p: a local coarse cell, its face (the opposite of the sender's fine face) and a child position 0 to 3; all three are -1 exactly where the sender's slot is empty.
All inputs are finite; a program needn't handle non-finite values.
Results may differ from a plain program's by a relative error of at most 0.0003.
Values sent between devices are 32-bit elements; how exact they have to be, the bound alone decides.
A program may use at most 128 MiB of HBM per device.

v0:
```python
import functools
import math

import jax
import jax.numpy as jnp
from jax import lax
from jax.experimental import pallas as pl
from jax.experimental.pallas import tpu as pltpu
from jax.sharding import PartitionSpec as P

LANES = 128
F32 = jnp.float32
BF16 = jnp.bfloat16
MESH = pl.DeviceIdType.MESH


def round_up(value, unit):
    return -(-value // unit) * unit


def split(x):
    hi = x.astype(BF16)
    lo = (x - hi.astype(F32)).astype(BF16)
    return hi, lo


def mm(a, b):
    return jnp.dot(a, b, preferred_element_type=F32)


def dot3(a_both, b_hi, b_lo):
    rows = a_both.shape[0] // 2
    first = mm(a_both, b_hi)
    return first[:rows] + first[rows:] + mm(a_both[:rows], b_lo)


def fill_flat(flat, refs, width):
    for at, ref in enumerate(refs):
        dofs, fields, cells = ref.shape
        used = dofs * fields
        for i in range(cells // LANES):
            for j in range(dofs):
                row = at * width + j * fields
                flat[i, row : row + fields, :] = ref[j, :, i * LANES : (i + 1) * LANES]
            flat[i, at * width + used : (at + 1) * width, :] = jnp.zeros((width - used, LANES), F32)


def lane_gather(blocks, lane, block_id):
    total = jnp.zeros(blocks[0].shape, F32)
    for i, block in enumerate(blocks):
        got = jnp.take_along_axis(block, lane, axis=1)
        total = jnp.where(block_id == i, got, total)
    return total


def exchange_kernel(
    dims,
    primal_ref,
    adjoint_ref,
    ghost_ref,
    edge_ref,
    hang_ref,
    from_gy,
    from_gx,
    to_gy,
    to_gx,
    ids,
    packed,
    flat,
    send_gy,
    recv_gy,
    send_gx,
    recv_gx,
):
    n_gx, n_gy, bits, ghosts, edges, hangs, fields, rows = dims
    gx = lax.axis_index("gx")
    gy = lax.axis_index("gy")
    dofs, _, cells = primal_ref.shape
    width = fields * rows
    partners = [jnp.bitwise_xor(gy, 1 << b) for b in range(bits)]

    barrier = pltpu.get_barrier_semaphore()
    for partner in partners:
        pl.semaphore_signal(barrier, inc=1, device_id=(gx, partner), device_id_type=MESH)

    @pl.when(gx > 0)
    def _():
        pl.semaphore_signal(barrier, inc=1, device_id=(gx - 1, gy), device_id_type=MESH)

    @pl.when(gx < n_gx - 1)
    def _():
        pl.semaphore_signal(barrier, inc=1, device_id=(gx + 1, gy), device_id_type=MESH)

    main = bits * ghosts + 2 * edges
    main_pad = round_up(main, LANES)
    hang_pad = round_up(bits * hangs, LANES)
    ids[...] = jnp.zeros_like(ids)
    for b, partner in enumerate(partners):
        ids[0:1, b * ghosts : (b + 1) * ghosts] = ghost_ref[0, pl.ds(partner, 1), :]
        at = main_pad + b * hangs
        ids[0:1, at : at + hangs] = hang_ref[0, 0, pl.ds(partner, 1), :]
    for side in range(2):
        at = bits * ghosts + side * edges
        ids[0:1, at : at + edges] = edge_ref[0, side : side + 1, :]
    fill_flat(flat, (primal_ref, adjoint_ref), width)
    chosen = jnp.maximum(ids[0:1, :], 0)
    for at in range(0, main_pad + hang_pad, LANES):
        part = jnp.broadcast_to(chosen[:, at : at + LANES], (rows, LANES))
        lane = jnp.bitwise_and(part, LANES - 1)
        block_id = jnp.right_shift(part, 7)
        count = 2 * fields if at < main_pad else fields
        for group in range(count):
            blocks = [flat[i, group * rows : (group + 1) * rows, :] for i in range(cells // LANES)]
            packed[group * rows : (group + 1) * rows, :] = lane_gather(blocks, lane, block_id)
        if at < main_pad:
            turned = packed[...].T
            for first in range(at, min(at + LANES, main), edges):
                chunk = turned[first - at : first - at + edges]
                if first < bits * ghosts:
                    inner = first % ghosts
                    to_gy[first // ghosts, inner : inner + edges, :] = chunk
                else:
                    to_gx[(first - bits * ghosts) // edges] = chunk
        else:
            turned = packed[0:width, :].T
            for b in range(bits):
                at_slot = b * hangs - (at - main_pad)
                if 0 <= at_slot < LANES:
                    to_gy[b, ghosts : ghosts + hangs, 0:width] = turned[at_slot : at_slot + hangs]
                    to_gy[b, ghosts : ghosts + hangs, width:] = jnp.zeros(
                        (hangs, to_gy.shape[2] - width), F32
                    )

    def low_copy():
        return pltpu.make_async_remote_copy(
            src_ref=to_gx.at[0],
            dst_ref=from_gx.at[1],
            send_sem=send_gx.at[0],
            recv_sem=recv_gx.at[1],
            device_id=(gx - 1, gy),
            device_id_type=MESH,
        )

    def high_copy():
        return pltpu.make_async_remote_copy(
            src_ref=to_gx.at[1],
            dst_ref=from_gx.at[0],
            send_sem=send_gx.at[1],
            recv_sem=recv_gx.at[0],
            device_id=(gx + 1, gy),
            device_id_type=MESH,
        )

    @pl.when((gx > 0) & (gx < n_gx - 1))
    def _():
        pl.semaphore_wait(barrier, bits + 2)

    @pl.when((gx == 0) | (gx == n_gx - 1))
    def _():
        pl.semaphore_wait(barrier, bits + (1 if n_gx > 1 else 0))

    copies = []
    for b in reversed(range(bits)):
        copy = pltpu.make_async_remote_copy(
            src_ref=to_gy.at[b],
            dst_ref=from_gy.at[b],
            send_sem=send_gy.at[b],
            recv_sem=recv_gy.at[b],
            device_id=(gx, partners[b]),
            device_id_type=MESH,
        )
        copy.start()
        copies.append(copy)

    @pl.when(gx > 0)
    def _():
        low_copy().start()

    @pl.when(gx == 0)
    def _():
        from_gx[0] = jnp.zeros(from_gx.shape[1:], F32)

    @pl.when(gx < n_gx - 1)
    def _():
        high_copy().start()

    @pl.when(gx == n_gx - 1)
    def _():
        from_gx[1] = jnp.zeros(from_gx.shape[1:], F32)

    for copy in copies:
        copy.wait()

    @pl.when(gx > 0)
    def _():
        low_copy().wait_send()
        high_copy().wait_recv()

    @pl.when(gx < n_gx - 1)
    def _():
        high_copy().wait_send()
        low_copy().wait_recv()


def compute_kernel(
    dims,
    primal_ref,
    adjoint_ref,
    source_ref,
    coef_ref,
    levels_ref,
    recon_ref,
    stiffness_ref,
    interp_ref,
    flux_ref,
    face_eval_ref,
    child_interp_ref,
    slot_ref,
    child_ref,
    hang_ref,
    from_gy,
    from_gx,
    cell_ref,
    face_ref,
    op_recon,
    op_res,
    op_face,
    op_child,
    child_flat,
    op_flux,
    op_map,
    maps,
    z_hi,
    z_lo,
    u_hi,
    u_lo,
    sources,
    flat,
    source_flat,
    hang_flat,
):
    n_gx, n_gy, bits, ghosts, edges, hangs, fields, rows = dims
    gy = lax.axis_index("gy")
    dofs, _, cells = primal_ref.shape
    quads = recon_ref.shape[2]
    own_blocks = cells // LANES
    width = fields * rows
    points = flux_ref.shape[1]
    remote = bits * ghosts + 2 * edges
    remote_pad = round_up(remote, LANES)
    hang_count = bits * hangs
    hang_pad = round_up(hang_count, LANES)
    hang_rows = round_up(hang_count, 16)
    children = 4

    op_recon[...] = jnp.zeros_like(op_recon)
    op_res[...] = jnp.zeros_like(op_res)
    op_face[...] = jnp.zeros_like(op_face)
    child_flat[...] = jnp.zeros_like(child_flat)
    op_flux[...] = jnp.zeros_like(op_flux)
    for j in range(dofs):
        op_recon[8 * j : 8 * j + 7, 0:quads] = recon_ref[j]
    op_res[0:dofs, 0:quads] = interp_ref[...]
    op_res[rows : rows + dofs, 0:quads] = stiffness_ref[...]
    for f in range(6):
        op_face[f * rows : f * rows + points, 0:quads] = face_eval_ref[f]
        op_flux[0:points, f * rows : f * rows + dofs] = flux_ref[f]
    for p in range(points):
        child_flat[children * p : children * (p + 1), 0:points] = child_interp_ref[p]
    for h in range(children):
        op_child[h * rows : (h + 1) * rows, :] = child_flat[pl.ds(h, rows, stride=children), :]
    flux_all = op_flux[...]
    flux_hi, flux_lo = split(flux_all)
    child_both = jnp.concatenate(split(op_child[...]), 0)
    mapped_ops = dot3(child_both[:, 0:rows], flux_hi, flux_lo)
    for f in range(6):
        opp = f ^ 1
        for h in range(children):
            op_map[f, :, h * rows : (h + 1) * rows] = mapped_ops[
                h * rows : (h + 1) * rows, opp * rows : (opp + 1) * rows
            ]
        op_map[f, :, 4 * rows : 5 * rows] = flux_all[:, opp * rows : (opp + 1) * rows]
        op_map[f, :, 5 * rows : 6 * rows] = flux_all[:, f * rows : (f + 1) * rows]
    recon_turned = [op_recon[pl.ds(f, rows, stride=8), :] for f in range(8)]
    recon_both = jnp.concatenate(split(jnp.concatenate(recon_turned, 0).T), 0)
    res_both = jnp.concatenate(split(op_res[...].T), 0)
    face_both = jnp.concatenate(split(op_face[...]), 0)
    flux_both = jnp.concatenate([flux_hi, flux_lo], 0)[:, 0 : 6 * rows]
    back_both = jnp.concatenate(split(op_child[...].T[0:rows]), 0)
    map_both = [jnp.concatenate(split(op_map[f]), 0) for f in range(6)]

    maps[...] = jnp.full(maps.shape, -1, jnp.int32)
    for b in range(bits):
        partner = jnp.bitwise_xor(gy, 1 << b)
        for i in range(3):
            maps[i : i + 1, b * hangs : (b + 1) * hangs] = hang_ref[i, 0, pl.ds(partner, 1), :]
    lane_face = maps[1:2, :]
    lane_child = maps[2:3, :]
    live = maps[0:1, :] >= 0
    place = jnp.where(live, maps[0:1, :] + lane_face * cells, -1).astype(F32)
    place_rows = jnp.broadcast_to(place, (LANES, hang_pad)).T[0:hang_rows, 0:1]

    fill_flat(flat, (primal_ref, adjoint_ref), width)
    fill_flat(source_flat, (source_ref,), width)
    parts = [from_gy[b, 0:ghosts, :] for b in range(bits)] + [from_gx[0], from_gx[1]]
    if remote_pad > remote:
        parts.append(jnp.zeros((remote_pad - remote, parts[0].shape[1]), F32))
    arrived = jnp.concatenate(parts, 0).T
    for i in range(remote_pad // LANES):
        flat[own_blocks + i] = arrived[:, i * LANES : (i + 1) * LANES]
    n_blocks = own_blocks + remote_pad // LANES
    for i in range(n_blocks):
        for group in range(2 * fields):
            first = group // fields * width + group % fields
            sources[i, group * rows : (group + 1) * rows, :] = flat[
                i, pl.ds(first, rows, stride=fields), :
            ]
    parts = [from_gy[b, ghosts : ghosts + hangs, 0:width] for b in range(bits)]
    parts.append(jnp.zeros((hang_pad - hang_count, width), F32))
    hang_flat[...] = jnp.concatenate(parts, 0).T

    slot = slot_ref[...]
    shifted = slot - cells
    log_ghosts = ghosts.bit_length() - 1
    peer = jnp.right_shift(shifted, log_ghosts)
    within = jnp.bitwise_and(shifted, ghosts - 1)
    differing = jnp.bitwise_xor(peer, gy)
    packed = jnp.zeros_like(slot)
    for b in range(1, bits):
        packed = jnp.where(differing == (1 << b), b, packed)
    slot = jnp.where(
        slot < cells,
        slot,
        jnp.where(
            shifted < n_gy * ghosts,
            cells + packed * ghosts + within,
            slot - (n_gy - bits) * ghosts,
        ),
    )
    for f in range(6):
        for at in range(0, cells, LANES):
            part = jnp.broadcast_to(slot[f : f + 1, at : at + LANES], (rows, LANES))
            lane = jnp.bitwise_and(part, LANES - 1)
            block_id = jnp.right_shift(part, 7)
            for group in range(2 * fields):
                blocks = [
                    sources[i, group * rows : (group + 1) * rows, :]
                    for i in range(n_blocks)
                ]
                hi, lo = split(lane_gather(blocks, lane, block_id))
                if group < fields:
                    u_hi[group, f, :, at : at + LANES] = hi
                    u_lo[group, f, :, at : at + LANES] = lo
                else:
                    k = group - fields
                    z_hi[k, f * rows : (f + 1) * rows, at : at + LANES] = hi
                    z_lo[k, f * rows : (f + 1) * rows, at : at + LANES] = lo

    column = lax.broadcasted_iota(jnp.int32, (hang_rows, cells), 1).astype(F32)
    place_wide = jnp.broadcast_to(place_rows, (hang_rows, cells))
    scatter = [
        jnp.where(place_wide == column + float(f * cells), 1.0, 0.0).astype(BF16) for f in range(6)
    ]
    coef = coef_ref[...]
    size = jnp.exp2(-levels_ref[...].astype(F32))
    zero = jnp.zeros((rows, cells), BF16)
    child_masks = []
    for f in range(6):
        wide = jnp.broadcast_to(child_ref[f : f + 1, :], (rows, cells))
        child_masks.append([wide == h for h in range(children + 1)])

    face_wide = jnp.broadcast_to(lane_face, (rows, hang_pad))
    child_wide = jnp.broadcast_to(lane_child, (rows, hang_pad))
    fine_masks = [face_wide == (f ^ 1) for f in range(6)]
    place_masks = [child_wide == h for h in range(children)]
    hang_zero = jnp.zeros((rows, hang_pad), BF16)

    for k in range(fields):
        own_u, own_z = [
            jnp.concatenate(
                [sources[i, at * rows : (at + 1) * rows, :] for i in range(own_blocks)], 1
            )
            for at in (k, fields + k)
        ]
        own_z_hi, own_z_lo = split(own_z)
        weight = dot3(
            recon_both[:, 0 : 7 * rows],
            jnp.concatenate([own_z_hi, z_hi[k]], 0),
            jnp.concatenate([own_z_lo, z_lo[k]], 0),
        )
        src_hi, src_lo = split(
            jnp.concatenate(
                [source_flat[i, pl.ds(k, rows, stride=fields), :] for i in range(own_blocks)], 1
            )
        )
        scaled_hi, scaled_lo = split(-coef * own_u)
        residual = dot3(
            res_both[:, 0 : 2 * rows],
            jnp.concatenate([src_hi, scaled_hi], 0),
            jnp.concatenate([src_lo, scaled_lo], 0),
        )
        cell_part = jnp.sum(residual * weight, axis=0, keepdims=True)
        cell_ref[k : k + 1, :] = size * cell_part * (1.0 / math.sqrt(quads))
        w_hi, w_lo = split(weight)
        face_weight = dot3(face_both, w_hi, w_lo)

        hang_parts = split(hang_flat[pl.ds(k, rows, stride=fields), :])
        hang_hi, hang_lo = [
            jnp.concatenate([jnp.where(m, x, hang_zero) for m in fine_masks], 0) for x in hang_parts
        ]
        trace_parts = split(dot3(flux_both, hang_hi, hang_lo))
        trace_hi, trace_lo = [
            jnp.concatenate([jnp.where(m, x, hang_zero) for m in place_masks], 0)
            for x in trace_parts
        ]
        traces = dot3(back_both, trace_hi, trace_lo)
        trace_both = jnp.concatenate(split(traces), 0)[:, 0:hang_rows]

        own_u_hi, own_u_lo = split(own_u)
        product = jnp.zeros((rows, cells), F32)
        for f in range(6):
            near_hi = u_hi[k, f]
            near_lo = u_lo[k, f]
            masks = child_masks[f]
            hi = jnp.concatenate([jnp.where(m, near_hi, zero) for m in masks] + [own_u_hi], 0)
            lo = jnp.concatenate([jnp.where(m, near_lo, zero) for m in masks] + [own_u_lo], 0)
            jump = dot3(map_both[f], hi, lo)
            extra = mm(trace_both, scatter[f])
            jump = jump + extra[0:rows] + extra[rows:]
            product = product + jump * face_weight[f * rows : (f + 1) * rows]
        face_part = jnp.sum(product, axis=0, keepdims=True)
        face_ref[k : k + 1, :] = size * face_part * (1.0 / math.sqrt(6 * points))


def solution(mesh):
    n_gx, n_gy = mesh.shape["gx"], mesh.shape["gy"]
    bits = n_gy.bit_length() - 1
    vmem = pl.BlockSpec(memory_space=pltpu.VMEM)

    def shards(
        primal,
        adjoint,
        source,
        coefficient,
        levels,
        recon,
        stiffness,
        interp,
        flux,
        face_eval,
        child_interp,
        ghost_send,
        edge_send,
        neighbor_slot,
        neighbor_child,
        hang_send,
        hang_recv,
    ):
        fields, dofs, cells = primal.shape
        ghosts, edges, hangs = ghost_send.shape[2], edge_send.shape[2], hang_send.shape[3]
        rows = round_up(dofs, 32)
        quads = recon.shape[1]
        quad_rows = round_up(quads, LANES)
        dims = (n_gx, n_gy, bits, ghosts, edges, hangs, fields, rows)
        primal, adjoint, source = [x.transpose(1, 0, 2) for x in (primal, adjoint, source)]
        main_pad = round_up(bits * ghosts + 2 * edges, LANES)
        hang_pad = round_up(bits * hangs, LANES)
        wide = 2 * fields * rows
        from_gy, from_gx = pl.pallas_call(
            functools.partial(exchange_kernel, dims),
            out_shape=(
                jax.ShapeDtypeStruct((bits, ghosts + hangs, wide), F32),
                jax.ShapeDtypeStruct((2, edges, wide), F32),
            ),
            in_specs=[vmem] * 5,
            out_specs=(vmem, vmem),
            scratch_shapes=[
                pltpu.VMEM((bits, ghosts + hangs, wide), F32),
                pltpu.VMEM((2, edges, wide), F32),
                pltpu.VMEM((8, main_pad + hang_pad), jnp.int32),
                pltpu.VMEM((wide, LANES), F32),
                pltpu.VMEM((cells // LANES, wide, LANES), F32),
                pltpu.SemaphoreType.DMA((bits,)),
                pltpu.SemaphoreType.DMA((bits,)),
                pltpu.SemaphoreType.DMA((2,)),
                pltpu.SemaphoreType.DMA((2,)),
            ],
            compiler_params=pltpu.CompilerParams(collective_id=0, has_side_effects=True),
            name="exchange",
        )(primal, adjoint, ghost_send, edge_send, hang_send)
        out = jax.ShapeDtypeStruct((fields, cells), F32)
        return pl.pallas_call(
            functools.partial(compute_kernel, dims),
            out_shape=(out, out),
            in_specs=[vmem] * 16,
            out_specs=(vmem, vmem),
            scratch_shapes=[
                pltpu.VMEM((8 * rows, quad_rows), F32),
                pltpu.VMEM((LANES, quad_rows), F32),
                pltpu.VMEM((6 * rows, quad_rows), F32),
                pltpu.VMEM((4 * rows, LANES), F32),
                pltpu.VMEM((4 * rows, LANES), F32),
                pltpu.VMEM((rows, round_up(6 * rows, LANES)), F32),
                pltpu.VMEM((6, rows, 6 * rows), F32),
                pltpu.VMEM((8, hang_pad), jnp.int32),
                pltpu.VMEM((fields, 6 * rows, cells), BF16),
                pltpu.VMEM((fields, 6 * rows, cells), BF16),
                pltpu.VMEM((fields, 6, rows, cells), BF16),
                pltpu.VMEM((fields, 6, rows, cells), BF16),
                pltpu.VMEM(((cells + main_pad) // LANES, wide, LANES), F32),
                pltpu.VMEM(((cells + main_pad) // LANES, wide, LANES), F32),
                pltpu.VMEM((cells // LANES, fields * rows, LANES), F32),
                pltpu.VMEM((fields * rows, hang_pad), F32),
            ],
            name="indicators",
        )(
            primal,
            adjoint,
            source,
            coefficient.reshape(1, cells),
            levels.reshape(1, cells),
            recon.transpose(2, 0, 1),
            stiffness.T,
            interp.T,
            flux,
            face_eval,
            child_interp.transpose(1, 0, 2),
            neighbor_slot,
            neighbor_child,
            hang_recv,
            from_gy,
            from_gx,
        )

    both = ("gx", "gy")
    placed = (
        P(None, None, both),
        P(None, None, both),
        P(None, None, both),
        P(both),
        P(both),
        P(),
        P(),
        P(),
        P(),
        P(),
        P(),
        P(both, None, None),
        P(both, None, None),
        P(None, both),
        P(None, both),
        P(None, both, None, None),
        P(None, both, None, None),
    )
    return jax.shard_map(
        shards,
        mesh=mesh,
        in_specs=placed,
        out_specs=(P(None, both), P(None, both)),
        check_vma=False,
    )
```

profile of v0, /device:TPU:0, one launch (start us, length us, event | category | flops | bytes accessed | tf_op | source)
XLA Modules:
  0.0 20.3 jit_solution(10437227619970736117)
XLA Ops:
  0.6 9.9 %exchange.1 = (f32[3,40,256]{2,1,0:T(8,128)}, f32[2,16,256]{2,1,0:T(8,128)}) custom-call(f32[27,4,512]{2,1,0:T(4,128)} %bitcast.9, f32[27,4,512]{2,1,0:T(4,128)} %bitcast.11, s32[1,8,32]{2,1,0:T(8,128)} %ghost_ref.1, s32[1,2,16]{2,1,0:T(2,128)} %edge_ref.1, s32[2,1,8,8]{3,2,1,0:T(8,128)} %hang_ref.2), custom_call_target="tpu_custom_call" | custom-call | tf_op jit(solution)/shard_map/exchange/pallas_call | solution.py:469
  10.5 9.7 %indicators.1 = (f32[4,512]{1,0:T(4,128)}, f32[4,512]{1,0:T(4,128)}) custom-call(f32[27,4,512]{2,1,0:T(4,128)} %bitcast.10, f32[27,4,512]{2,1,0:T(4,128)} %bitcast.12, f32[27,4,512]{2,1,0:T(4,128)} %bitcast.13, f32[1,512]{1,0:T(1,128)} %bitcast.18, s32[1,512]{1,0:T(1,128)} %bitcast.19, f32[27,7,125]{2,1,0:T(8,128)} %bitcast.14, f32[27,125]{1,0:T(8,128)} %bitcast.16, ...), custom_call_target="tpu_custom_call" | custom-call | tf_op jit(solution)/shard_map/indicators/pallas_call | solution.py:492
where the time goes:
time: 20.4 us; the launch traced here: 20.3 us
  Pallas kernels  19.6 us (96%)
  between operations  0.64 us (3%)
    pallas_call x1, Pallas kernels, shards(): pl.pallas_call(functools.partial(exchange_kernel, dims), out_shape=(jax.S...  9.89 us
    pallas_call x1, Pallas kernels, shards(): pl.pallas_call(functools.partial(compute_kernel, dims), out_shape=(out, o...  9.75 us

commit v1 on v0

--- a/solution.py
+++ b/solution.py
@@ -53,20 +53,51 @@
     return total
 
 
-def exchange_kernel(
+def compute_kernel(
     dims,
     primal_ref,
     adjoint_ref,
+    source_ref,
+    coef_ref,
+    levels_ref,
+    recon_ref,
+    stiffness_ref,
+    interp_ref,
+    flux_ref,
+    face_eval_ref,
+    child_interp_ref,
+    slot_ref,
+    child_ref,
+    hang_ref,
     ghost_ref,
     edge_ref,
-    hang_ref,
+    hang_send_ref,
+    cell_ref,
+    face_ref,
+    op_recon,
+    op_res,
+    op_face,
+    op_child,
+    child_flat,
+    op_flux,
+    op_map,
+    maps,
+    z_hi,
+    z_lo,
+    u_hi,
+    u_lo,
+    sources,
+    flat,
+    source_flat,
+    hang_flat,
+    near,
+    residuals,
     from_gy,
     from_gx,
     to_gy,
     to_gx,
     ids,
     packed,
-    flat,
     send_gy,
     recv_gy,
     send_gx,
@@ -98,7 +129,7 @@
     for b, partner in enumerate(partners):
         ids[0:1, b * ghosts : (b + 1) * ghosts] = ghost_ref[0, pl.ds(partner, 1), :]
         at = main_pad + b * hangs
-        ids[0:1, at : at + hangs] = hang_ref[0, 0, pl.ds(partner, 1), :]
+        ids[0:1, at : at + hangs] = hang_send_ref[0, 0, pl.ds(partner, 1), :]
     for side in range(2):
         at = bits * ghosts + side * edges
         ids[0:1, at : at + edges] = edge_ref[0, side : side + 1, :]
@@ -188,63 +219,8 @@
     def _():
         from_gx[1] = jnp.zeros(from_gx.shape[1:], F32)
 
-    for copy in copies:
-        copy.wait()
-
-    @pl.when(gx > 0)
-    def _():
-        low_copy().wait_send()
-        high_copy().wait_recv()
-
-    @pl.when(gx < n_gx - 1)
-    def _():
-        high_copy().wait_send()
-        low_copy().wait_recv()
-
-
-def compute_kernel(
-    dims,
-    primal_ref,
-    adjoint_ref,
-    source_ref,
-    coef_ref,
-    levels_ref,
-    recon_ref,
-    stiffness_ref,
-    interp_ref,
-    flux_ref,
-    face_eval_ref,
-    child_interp_ref,
-    slot_ref,
-    child_ref,
-    hang_ref,
-    from_gy,
-    from_gx,
-    cell_ref,
-    face_ref,
-    op_recon,
-    op_res,
-    op_face,
-    op_child,
-    child_flat,
-    op_flux,
-    op_map,
-    maps,
-    z_hi,
-    z_lo,
-    u_hi,
-    u_lo,
-    sources,
-    flat,
-    source_flat,
-    hang_flat,
-):
-    n_gx, n_gy, bits, ghosts, edges, hangs, fields, rows = dims
-    gy = lax.axis_index("gy")
-    dofs, _, cells = primal_ref.shape
     quads = recon_ref.shape[2]
     own_blocks = cells // LANES
-    width = fields * rows
     points = flux_ref.shape[1]
     remote = bits * ghosts + 2 * edges
     remote_pad = round_up(remote, LANES)
@@ -300,8 +276,72 @@
     place = jnp.where(live, maps[0:1, :] + lane_face * cells, -1).astype(F32)
     place_rows = jnp.broadcast_to(place, (LANES, hang_pad)).T[0:hang_rows, 0:1]
 
-    fill_flat(flat, (primal_ref, adjoint_ref), width)
     fill_flat(source_flat, (source_ref,), width)
+    for i in range(own_blocks):
+        for group in range(2 * fields):
+            first = group // fields * width + group % fields
+            sources[i, group * rows : (group + 1) * rows, :] = flat[
+                i, pl.ds(first, rows, stride=fields), :
+            ]
+
+    slot = slot_ref[...]
+    shifted = slot - cells
+    log_ghosts = ghosts.bit_length() - 1
+    peer = jnp.right_shift(shifted, log_ghosts)
+    within = jnp.bitwise_and(shifted, ghosts - 1)
+    differing = jnp.bitwise_xor(peer, gy)
+    place_of = jnp.zeros_like(slot)
+    for b in range(1, bits):
+        place_of = jnp.where(differing == (1 << b), b, place_of)
+    slot = jnp.where(
+        slot < cells,
+        slot,
+        jnp.where(
+            shifted < n_gy * ghosts,
+            cells + place_of * ghosts + within,
+            slot - (n_gy - bits) * ghosts,
+        ),
+    )
+    coef = coef_ref[...]
+    for k in range(fields):
+        own_u = jnp.concatenate(
+            [sources[i, k * rows : (k + 1) * rows, :] for i in range(own_blocks)], 1
+        )
+        src_hi, src_lo = split(
+            jnp.concatenate(
+                [source_flat[i, pl.ds(k, rows, stride=fields), :] for i in range(own_blocks)], 1
+            )
+        )
+        scaled_hi, scaled_lo = split(-coef * own_u)
+        residuals[k] = dot3(
+            res_both[:, 0 : 2 * rows],
+            jnp.concatenate([src_hi, scaled_hi], 0),
+            jnp.concatenate([src_lo, scaled_lo], 0),
+        )
+
+    for f in range(6):
+        for at in range(0, cells, LANES):
+            part = jnp.broadcast_to(slot[f : f + 1, at : at + LANES], (rows, LANES))
+            lane = jnp.bitwise_and(part, LANES - 1)
+            block_id = jnp.right_shift(part, 7)
+            for group in range(2 * fields):
+                span = slice(group * rows, (group + 1) * rows)
+                blocks = [sources[i, span, :] for i in range(own_blocks)]
+                near[f, at // LANES, span, :] = lane_gather(blocks, lane, block_id)
+
+    for copy in copies:
+        copy.wait()
+
+    @pl.when(gx > 0)
+    def _():
+        low_copy().wait_send()
+        high_copy().wait_recv()
+
+    @pl.when(gx < n_gx - 1)
+    def _():
+        high_copy().wait_send()
+        low_copy().wait_recv()
+
     parts = [from_gy[b, 0:ghosts, :] for b in range(bits)] + [from_gx[0], from_gx[1]]
     if remote_pad > remote:
         parts.append(jnp.zeros((remote_pad - remote, parts[0].shape[1]), F32))
@@ -309,7 +349,7 @@
     for i in range(remote_pad // LANES):
         flat[own_blocks + i] = arrived[:, i * LANES : (i + 1) * LANES]
     n_blocks = own_blocks + remote_pad // LANES
-    for i in range(n_blocks):
+    for i in range(own_blocks, n_blocks):
         for group in range(2 * fields):
             first = group // fields * width + group % fields
             sources[i, group * rows : (group + 1) * rows, :] = flat[
@@ -319,35 +359,18 @@
     parts.append(jnp.zeros((hang_pad - hang_count, width), F32))
     hang_flat[...] = jnp.concatenate(parts, 0).T
 
-    slot = slot_ref[...]
-    shifted = slot - cells
-    log_ghosts = ghosts.bit_length() - 1
-    peer = jnp.right_shift(shifted, log_ghosts)
-    within = jnp.bitwise_and(shifted, ghosts - 1)
-    differing = jnp.bitwise_xor(peer, gy)
-    packed = jnp.zeros_like(slot)
-    for b in range(1, bits):
-        packed = jnp.where(differing == (1 << b), b, packed)
-    slot = jnp.where(
-        slot < cells,
-        slot,
-        jnp.where(
-            shifted < n_gy * ghosts,
-            cells + packed * ghosts + within,
-            slot - (n_gy - bits) * ghosts,
-        ),
-    )
     for f in range(6):
         for at in range(0, cells, LANES):
             part = jnp.broadcast_to(slot[f : f + 1, at : at + LANES], (rows, LANES))
             lane = jnp.bitwise_and(part, LANES - 1)
             block_id = jnp.right_shift(part, 7)
             for group in range(2 * fields):
-                blocks = [
-                    sources[i, group * rows : (group + 1) * rows, :]
-                    for i in range(n_blocks)
-                ]
-                hi, lo = split(lane_gather(blocks, lane, block_id))
+                span = slice(group * rows, (group + 1) * rows)
+                total = near[f, at // LANES, span, :]
+                for i in range(own_blocks, n_blocks):
+                    got = jnp.take_along_axis(sources[i, span, :], lane, axis=1)
+                    total = jnp.where(block_id == i, got, total)
+                hi, lo = split(total)
                 if group < fields:
                     u_hi[group, f, :, at : at + LANES] = hi
                     u_lo[group, f, :, at : at + LANES] = lo
@@ -361,7 +384,6 @@
     scatter = [
         jnp.where(place_wide == column + float(f * cells), 1.0, 0.0).astype(BF16) for f in range(6)
     ]
-    coef = coef_ref[...]
     size = jnp.exp2(-levels_ref[...].astype(F32))
     zero = jnp.zeros((rows, cells), BF16)
     child_masks = []
@@ -388,17 +410,7 @@
             jnp.concatenate([own_z_hi, z_hi[k]], 0),
             jnp.concatenate([own_z_lo, z_lo[k]], 0),
         )
-        src_hi, src_lo = split(
-            jnp.concatenate(
-                [source_flat[i, pl.ds(k, rows, stride=fields), :] for i in range(own_blocks)], 1
-            )
-        )
-        scaled_hi, scaled_lo = split(-coef * own_u)
-        residual = dot3(
-            res_both[:, 0 : 2 * rows],
-            jnp.concatenate([src_hi, scaled_hi], 0),
-            jnp.concatenate([src_lo, scaled_lo], 0),
-        )
+        residual = residuals[k]
         cell_part = jnp.sum(residual * weight, axis=0, keepdims=True)
         cell_ref[k : k + 1, :] = size * cell_part * (1.0 / math.sqrt(quads))
         w_hi, w_lo = split(weight)
@@ -466,33 +478,11 @@
         main_pad = round_up(bits * ghosts + 2 * edges, LANES)
         hang_pad = round_up(bits * hangs, LANES)
         wide = 2 * fields * rows
-        from_gy, from_gx = pl.pallas_call(
-            functools.partial(exchange_kernel, dims),
-            out_shape=(
-                jax.ShapeDtypeStruct((bits, ghosts + hangs, wide), F32),
-                jax.ShapeDtypeStruct((2, edges, wide), F32),
-            ),
-            in_specs=[vmem] * 5,
-            out_specs=(vmem, vmem),
-            scratch_shapes=[
-                pltpu.VMEM((bits, ghosts + hangs, wide), F32),
-                pltpu.VMEM((2, edges, wide), F32),
-                pltpu.VMEM((8, main_pad + hang_pad), jnp.int32),
-                pltpu.VMEM((wide, LANES), F32),
-                pltpu.VMEM((cells // LANES, wide, LANES), F32),
-                pltpu.SemaphoreType.DMA((bits,)),
-                pltpu.SemaphoreType.DMA((bits,)),
-                pltpu.SemaphoreType.DMA((2,)),
-                pltpu.SemaphoreType.DMA((2,)),
-            ],
-            compiler_params=pltpu.CompilerParams(collective_id=0, has_side_effects=True),
-            name="exchange",
-        )(primal, adjoint, ghost_send, edge_send, hang_send)
         out = jax.ShapeDtypeStruct((fields, cells), F32)
         return pl.pallas_call(
             functools.partial(compute_kernel, dims),
             out_shape=(out, out),
-            in_specs=[vmem] * 16,
+            in_specs=[vmem] * 17,
             out_specs=(vmem, vmem),
             scratch_shapes=[
                 pltpu.VMEM((8 * rows, quad_rows), F32),
@@ -511,7 +501,20 @@
                 pltpu.VMEM(((cells + main_pad) // LANES, wide, LANES), F32),
                 pltpu.VMEM((cells // LANES, fields * rows, LANES), F32),
                 pltpu.VMEM((fields * rows, hang_pad), F32),
+                pltpu.VMEM((6, cells // LANES, wide, LANES), F32),
+                pltpu.VMEM((fields, quad_rows, cells), F32),
+                pltpu.VMEM((bits, ghosts + hangs, wide), F32),
+                pltpu.VMEM((2, edges, wide), F32),
+                pltpu.VMEM((bits, ghosts + hangs, wide), F32),
+                pltpu.VMEM((2, edges, wide), F32),
+                pltpu.VMEM((8, main_pad + hang_pad), jnp.int32),
+                pltpu.VMEM((wide, LANES), F32),
+                pltpu.SemaphoreType.DMA((bits,)),
+                pltpu.SemaphoreType.DMA((bits,)),
+                pltpu.SemaphoreType.DMA((2,)),
+                pltpu.SemaphoreType.DMA((2,)),
             ],
+            compiler_params=pltpu.CompilerParams(collective_id=0, has_side_effects=True),
             name="indicators",
         )(
             primal,
@@ -528,8 +531,9 @@
             neighbor_slot,
             neighbor_child,
             hang_recv,
-            from_gy,
-            from_gx,
+            ghost_send,
+            edge_send,
+            hang_send,
         )
 
     both = ("gx", "gy")

time: 20.4 us -> 17.8 us (0.87)
  Pallas kernels: 19.6 us -> 15 us
  local copies, waits for them, and re-layouts: 0 us -> 1.9 us
    pallas_call x1 -> x0, Pallas kernels: 9.89 us -> none  [shards(): pl.pallas_call(functools.partial(exchange_kernel, dims), out_shape=(jax.S...]
    pallas_call x1, Pallas kernels: 9.75 us -> 15 us  [shards(): pl.pallas_call(functools.partial(compute_kernel, dims), out_shape=(out, o...]
    unnamed x0 -> x4, local copies, waits for them, and re-layouts: none -> 1.9 us
where the time goes in v1:
time: 17.8 us; the launch traced here: 17.6 us
  Pallas kernels  15 us (84%)
  local copies, waits for them, and re-layouts  1.9 us (11%)
  between operations  0.65 us (4%)
    pallas_call x1, Pallas kernels, shards(): pl.pallas_call(functools.partial(compute_kernel, dims), out_shape=(out, o...  15 us
    unnamed x4, local copies, waits for them, and re-layouts  1.9 us

profile of v1, /device:TPU:0, one launch (start us, length us, event | category | flops | bytes accessed | tf_op | source)
XLA Modules:
  0.0 17.6 jit_solution(3404756229690446966)
XLA Ops:
  0.6 15.0 %indicators.1 = (f32[4,512]{1,0:T(4,128)}, f32[4,512]{1,0:T(4,128)}) custom-call(f32[27,4,512]{2,1,0:T(4,128)} %bitcast.9, f32[27,4,512]{2,1,0:T(4,128)} %bitcast.10, f32[27,4,512]{2,1,0:T(4,128)} %bitcast.11, f32[1,512]{1,0:T(1,128)} %bitcast.16, s32[1,512]{1,0:T(1,128)} %bitcast.17, f32[27,7,125]{2,1,0:T(8,128)} %bitcast.12, f32[27,125]{1,0:T(8,128)} %bitcast.14, ...), custom_call_target="tpu_custom_call" | custom-call | tf_op jit(solution)/shard_map/indicators/pallas_call | solution.py:482
  15.7 0.0 copy-start
  15.7 1.3 %copy.21 = f32[4,512]{1,0:T(4,128)} copy(f32[4,512]{1,0:T(4,128)} %get-tuple-element.4) | data formatting | bytes 16384
  17.0 0.0 copy-done
  17.0 0.6 %copy.22 = f32[4,512]{1,0:T(4,128)} copy(f32[4,512]{1,0:T(4,128)S(1)} %copy-done) | data formatting | bytes 16384
Async XLA Ops:
  15.7 1.3 %copy-start = (f32[4,512]{1,0:T(4,128)S(1)}, f32[4,512]{1,0:T(4,128)}, u32[]{:S(2)}) copy-start(f32[4,512]{1,0:T(4,128)} %get-tuple-element.5) | copy-start | bytes 24580
